TPU v7x, 32 devices: a whole 2x2x4 slice. The times are simulated.
32 devices in a mesh: mkt: 4 (over z), draw: 4 (over y, core), nest: 2 (over x).
Axes of the slice: x: 2, y: 2, z: 4, core: 2. Of those that a mesh axis runs over, the one named last changes fastest.
Arguments:
- features: bfloat16 [32, 512, 128], P(None, 'mkt'), may hold values from -1.5 to 1.5
- taste_draws: bfloat16 [128, 32, 512], P('mkt', None, 'draw'), may hold values from -4 to 4
- taste_scale: float32 [32], replicated, may hold values from 0.2 to 1
- nest_param: float32 [16], P('nest'), may hold values from 0.3 to 0.95
- members: int32 [16, 48], P('nest'), may hold values from -1 to 511, as said below
- log_share: float32 [512, 128], P('mkt'), may hold values from -10 to -7
Outputs:
- mean_utility: float32 [128, 768], P('mkt', 'nest')
- model_share: float32 [128, 768], P('mkt', 'nest')
Inputs may be any that keep to these rules, and one draw needn't show every extreme that they name: `members`: every product id 0 to 511 stands in exactly one slot; in each nest's row the ids fill the first slots and -1 fills the rest; each nest holds at least 16 products, and some nest fills all 48 slots.
All inputs are finite; a program needn't handle non-finite values.
Results may differ from a plain program's by a relative error of at most 0.0013.
The roundings to bfloat16 on the way count: a program that leaves them out, or rounds other values in their place, can miss the bound.
Values may be sent and summed in bfloat16 or wider, within the bound.
A program may use at most 64 MiB of HBM per device.

v0:
```python
import jax
import jax.numpy as jnp
from jax import lax
from jax.sharding import PartitionSpec as P

ITERS = 3


def revise(value_slot, slot_share, target, nest_rate, occupied):
    safe_share = jnp.where(occupied[None, :], slot_share, 1.0)
    moved_value = value_slot + (1.0 - nest_rate)[None, :] * (target - jnp.log(safe_share))
    return jnp.where(occupied[None, :], moved_value, 0.0)


def shards(features, taste_draws, taste_scale, nest_param, members, log_share):
    market_x = lax.all_to_all(features, "mkt", split_axis=2, concat_axis=1, tiled=True)
    market_log = lax.all_to_all(log_share, "mkt", split_axis=1, concat_axis=0, tiled=True)
    market_list = market_log.shape[1]
    product_count = market_log.shape[0]
    nest_count = members.shape[0]
    slot_count = members.shape[1]
    columns = nest_count * slot_count
    draws_here = taste_draws.shape[2]
    total_draws = draws_here * lax.axis_size("draw")
    product_ids = members.reshape(columns)
    occupied = product_ids >= 0
    safe_ids = jnp.maximum(product_ids, 0)
    live_flag = occupied.astype(jnp.float32)
    product_range = jnp.arange(product_count, dtype=jnp.int32)
    onehot = ((safe_ids[None, :] == product_range[:, None]) & occupied[None, :]).astype(
        jnp.bfloat16
    )
    slot_features = jnp.einsum(
        "kjm,js->mks", market_x, onehot, preferred_element_type=jnp.float32
    ).astype(jnp.bfloat16)
    slot_log = jnp.transpose(jnp.take(market_log, safe_ids, axis=0), (1, 0))
    outside = 1.0 - jnp.sum(jnp.exp(market_log), axis=0)
    value_slot = jnp.where(occupied[None, :], slot_log - jnp.log(outside)[:, None], 0.0)
    taste_matrix = (taste_scale[None, :, None] * taste_draws.astype(jnp.float32)).astype(
        jnp.bfloat16
    )
    nest_rate = jnp.repeat(nest_param, slot_count)
    mean_utility_part = jnp.einsum(
        "dve,dvb->deb", slot_features, taste_matrix, preferred_element_type=jnp.float32
    )
    slot_share = jnp.zeros_like(value_slot)
    for iteration in range(ITERS):
        utility = live_flag[None, :, None] * jnp.exp(
            (value_slot[:, :, None] + mean_utility_part) / nest_rate[None, :, None]
        )
        grouped = utility.reshape(market_list, nest_count, slot_count, draws_here)
        inner_sum = jnp.sum(grouped, axis=2)
        inclusive_value = jnp.exp(nest_param[None, :, None] * jnp.log(inner_sum))
        totals = lax.psum(jnp.sum(inclusive_value, axis=1), "nest")
        nest_ratio = inclusive_value / (inner_sum * (1.0 + totals)[:, None, :])
        share_terms = jnp.sum(grouped * nest_ratio[:, :, None, :], axis=3).reshape(
            market_list, columns
        )
        slot_share = lax.psum(share_terms, "draw") / total_draws
        value_slot = revise(value_slot, slot_share, slot_log, nest_rate, occupied)
    return (value_slot, slot_share)


def solution(mesh):
    in_specs = (
        P(None, "mkt", None),
        P("mkt", None, "draw"),
        P(),
        P("nest"),
        P("nest", None),
        P("mkt", None),
    )
    out_specs = (P("mkt", "nest"), P("mkt", "nest"))
    return jax.shard_map(shards, mesh=mesh, in_specs=in_specs, out_specs=out_specs, check_vma=False)
```

profile of v0, /device:TPU:1, one launch (start us, length us, event | category | flops | bytes accessed | tf_op | source)
XLA Modules:
  0.0 170.8 jit_solution(5884183083681372627)
XLA Ops:
  0.7 1.6 copy.23
  2.2 5.4 %all-to-all-start = ((f32[128,4,32]{0,2,1:T(8,128)}), f32[128,4,32]{0,2,1:T(8,128)S(1)}, u32[]{:S(2)}, u32[]{:S(2)}) async-start(f32[128,4,32]{0,2,1:T(8,128)} %bitcast), calls=%async_computation | async-start | bytes 131072 | tf_op jit(solution)/shard_map/all_to_all | solution.py:17
  8.5 2.7 %copy.26 = bf16[32,128,128]{1,0,2:T(8,128)(2,1)} copy(bf16[32,128,128]{2,1,0:T(8,128)(2,1)} %param.6) | data formatting | bytes 2097152 | tf_op args[0]
  12.3 3.5 %all-to-all-start.1 = ((bf16[32,128,128]{1,0,2:T(8,128)(2,1)}), bf16[32,128,128]{1,0,2:T(8,128)(2,1)S(1)}, u32[]{:S(2)}, u32[]{:S(2)}) async-start(bf16[32,128,128]{1,0,2:T(8,128)(2,1)} %copy.26), calls=%async_computation.1 | async-start | bytes 2097152 | tf_op jit(solution)/shard_map/all_to_all | solution.py:16
  17.5 1.1 gather_fusion
  19.1 22.0 %all-to-all-done.1 = bf16[32,128,128]{1,0,2:T(8,128)(2,1)S(1)} async-done(((bf16[32,128,128]{1,0,2:T(8,128)(2,1)}), bf16[32,128,128]{1,0,2:T(8,128)(2,1)S(1)}, u32[]{:S(2)}, u32[]{:S(2)}) %all-to-all-start.1) | async-done | bytes 1048608 | tf_op jit(solution)/shard_map/all_to_all | solution.py:16
  41.0 6.5 %exponential_multiply_fusion.2 = (f32[32,384,128]{2,1,0:T(8,128)}, f32[32,384,128]{2,1,0:T(8,128)}) fusion(f32[384]{0:T(512)S(1)} %reshape.109, f32[32,384]{1,0:T(8,128)S(1)} %copy.25, f32[384]{0:T(512)S(1)} %convert_element_type.20, bf16[32,32,128]{2,1,0:T(8,128)(2,1)S(1)} %copy-done.1, f32[32]{0:T(128)S(1)} %copy-done.2, ...), kind=kOutput, calls=%fused_computation.6 | convolution fusion | flops 509214720 | bytes 13947904 | tf_op jit(solution)/shard_map/dve,dvb->deb/dot_general | solution.py:43
  47.5 3.7 %reduce_sum.91 = f32[32,8,128]{2,1,0:T(8,128)S(1)} reduce(f32[32,8,48,128]{3,2,1,0:T(8,128)} %bitcast.62, f32[]{:T(128)} %constant.28.clone.1), dimensions={2}, to_apply=%region_1.2 | reduce | flops 1540096 | bytes 6422532 | tf_op jit(solution)/shard_map/reduce_sum | solution.py:52
  51.3 6.1 %psum.42 = f32[32,128]{1,0:T(8,128)S(1)} all-reduce(f32[32,128]{1,0:T(8,128)S(1)} %fusion.27), channel_id=1, replica_groups=mesh['mkt'=4,'draw'=4,'nest'=2] {'nest'}, use_global_device_ids=true, to_apply=%region_3.4 | all-reduce | flops 4096 | bytes 32768 | tf_op jit(solution)/shard_map/psum | solution.py:54
  57.5 6.2 %bitcast_multiply_fusion.2 = f32[32,384,128]{2,1,0:T(8,128)} fusion(f32[32,384,128]{2,1,0:T(8,128)} %get-tuple-element.10, f32[32,8,128]{2,1,0:T(8,128)S(1)} %multiply_divide_fusion.2), kind=kLoop, calls=%fused_computation.3 | loop fusion | flops 1572864 | bytes 12713984 | tf_op jit(solution)/shard_map/mul | solution.py:56
  63.8 4.5 %reduce_sum.93 = f32[32,384]{1,0:T(8,128)S(1)} reduce(f32[32,384,128]{2,1,0:T(8,128)} %bitcast_multiply_fusion.2, f32[]{:T(128)} %constant.28.clone.1), dimensions={2}, to_apply=%region_4.5 | reduce | flops 1560576 | bytes 6340612 | tf_op jit(solution)/shard_map/reduce_sum | solution.py:56
  68.4 15.4 %psum.43 = f32[32,384]{0,1:T(8,128)S(1)} all-reduce(f32[32,384]{0,1:T(8,128)S(1)} %copy.30), channel_id=1, replica_groups=mesh['mkt'=4,'draw'=4,'nest'=2] {'draw'}, use_global_device_ids=true, to_apply=%region_5.6 | all-reduce | flops 12288 | bytes 98304 | tf_op jit(solution)/shard_map/psum | solution.py:59
  84.1 6.8 %exponential_multiply_fusion.1 = f32[32,384,128]{2,1,0:T(8,128)} fusion(f32[32,384,128]{2,1,0:T(8,128)} %get-tuple-element.11, f32[32,384]{1,0:T(8,128)S(1)} %copy.31, f32[384]{0:T(512)S(1)} %reshape.109, f32[384]{0:T(512)S(1)} %convert_element_type.20), kind=kLoop, calls=%fused_computation.5 | loop fusion | flops 4718592 | bytes 12635136 | tf_op jit(solution)/shard_map/mul | solution.py:48
  90.9 3.7 %reduce_sum.94 = f32[32,8,128]{2,1,0:T(8,128)S(1)} reduce(f32[32,8,48,128]{3,2,1,0:T(8,128)} %bitcast.63, f32[]{:T(128)} %constant.28.clone.1), dimensions={2}, to_apply=%region_6.7 | reduce | flops 1540096 | bytes 6422532 | tf_op jit(solution)/shard_map/reduce_sum | solution.py:52
  94.6 5.2 %psum.44 = f32[32,128]{1,0:T(8,128)S(1)} all-reduce(f32[32,128]{1,0:T(8,128)S(1)} %fusion.26), channel_id=1, replica_groups=mesh['mkt'=4,'draw'=4,'nest'=2] {'nest'}, use_global_device_ids=true, to_apply=%region_8.9 | all-reduce | flops 4096 | bytes 32768 | tf_op jit(solution)/shard_map/psum | solution.py:54
  99.9 6.9 %bitcast_multiply_fusion.1 = f32[32,384,128]{2,1,0:T(8,128)} fusion(f32[32,8,128]{2,1,0:T(8,128)S(1)} %multiply_divide_fusion.1, f32[384]{0:T(512)S(1)} %reshape.109, f32[32,384,128]{2,1,0:T(8,128)} %get-tuple-element.11, f32[32,384]{1,0:T(8,128)S(1)} %copy.31, f32[384]{0:T(512)S(1)} %convert_element_type.20), kind=kLoop, calls=%fused_computation.2 | loop fusion | flops 6291456 | bytes 12766208 | tf_op jit(solution)/shard_map/mul | solution.py:56
  106.9 4.5 %reduce_sum.96 = f32[32,384]{1,0:T(8,128)S(1)} reduce(f32[32,384,128]{2,1,0:T(8,128)} %bitcast_multiply_fusion.1, f32[]{:T(128)} %constant.28.clone.1), dimensions={2}, to_apply=%region_9.10 | reduce | flops 1560576 | bytes 6340612 | tf_op jit(solution)/shard_map/reduce_sum | solution.py:56
  111.5 14.6 %psum.45 = f32[32,384]{0,1:T(8,128)S(1)} all-reduce(f32[32,384]{0,1:T(8,128)S(1)} %copy.32), channel_id=1, replica_groups=mesh['mkt'=4,'draw'=4,'nest'=2] {'draw'}, use_global_device_ids=true, to_apply=%region_10.11 | all-reduce | flops 12288 | bytes 98304 | tf_op jit(solution)/shard_map/psum | solution.py:59
  126.4 6.8 %exponential_multiply_fusion = f32[32,384,128]{2,1,0:T(8,128)} fusion(f32[32,384,128]{2,1,0:T(8,128)} %get-tuple-element.11, f32[32,384]{1,0:T(8,128)S(1)} %copy.33, f32[384]{0:T(512)S(1)} %reshape.109, f32[384]{0:T(512)S(1)} %convert_element_type.20), kind=kLoop, calls=%fused_computation.4 | loop fusion | flops 4718592 | bytes 12635136 | tf_op jit(solution)/shard_map/mul | solution.py:48
  133.2 3.7 %reduce_sum.97 = f32[32,8,128]{2,1,0:T(8,128)S(1)} reduce(f32[32,8,48,128]{3,2,1,0:T(8,128)} %bitcast.64, f32[]{:T(128)} %constant.28.clone.1), dimensions={2}, to_apply=%region_11.12 | reduce | flops 1540096 | bytes 6422532 | tf_op jit(solution)/shard_map/reduce_sum | solution.py:52
  137.0 6.1 %psum.46 = f32[32,128]{1,0:T(8,128)S(1)} all-reduce(f32[32,128]{1,0:T(8,128)S(1)} %fusion.25), channel_id=1, replica_groups=mesh['mkt'=4,'draw'=4,'nest'=2] {'nest'}, use_global_device_ids=true, to_apply=%region_13.14 | all-reduce | flops 4096 | bytes 32768 | tf_op jit(solution)/shard_map/psum | solution.py:54
  143.2 6.9 %bitcast_multiply_fusion = f32[32,384,128]{2,1,0:T(8,128)} fusion(f32[32,8,128]{2,1,0:T(8,128)S(1)} %multiply_divide_fusion, f32[384]{0:T(512)S(1)} %reshape.109, f32[32,384,128]{2,1,0:T(8,128)} %get-tuple-element.11, f32[32,384]{1,0:T(8,128)S(1)} %copy.33, f32[384]{0:T(512)S(1)} %convert_element_type.20), kind=kLoop, calls=%fused_computation.1 | loop fusion | flops 6291456 | bytes 12766208 | tf_op jit(solution)/shard_map/mul | solution.py:56
  150.1 4.5 %reduce_sum.99 = f32[32,384]{1,0:T(8,128)S(1)} reduce(f32[32,384,128]{2,1,0:T(8,128)} %bitcast_multiply_fusion, f32[]{:T(128)} %constant.28.clone.1), dimensions={2}, to_apply=%region_14.15 | reduce | flops 1560576 | bytes 6340612 | tf_op jit(solution)/shard_map/reduce_sum | solution.py:56
  154.7 14.4 %psum.47 = f32[32,384]{0,1:T(8,128)S(1)} all-reduce(f32[32,384]{0,1:T(8,128)S(1)} %copy.34), channel_id=1, replica_groups=mesh['mkt'=4,'draw'=4,'nest'=2] {'draw'}, use_global_device_ids=true, to_apply=%region_15.16 | all-reduce | flops 12288 | bytes 98304 | tf_op jit(solution)/shard_map/psum | solution.py:59
  (41 shorter events, 7.4 us)
Async XLA Ops:
  0.6 40.4 %copy-start.1 = (bf16[32,32,128]{2,1,0:T(8,128)(2,1)S(1)}, bf16[32,32,128]{2,1,0:T(8,128)(2,1)}, u32[]{:S(2)}) copy-start(bf16[32,32,128]{2,1,0:T(8,128)(2,1)} %param.7) | copy-start | bytes 786436
  0.6 40.4 %copy-start.2 = (f32[32]{0:T(128)S(1)}, f32[32]{0:T(128)}, u32[]{:S(2)}) copy-start(f32[32]{0:T(128)} %param.8) | copy-start | bytes 388
  2.2 10.0 %all-to-all-start = ((f32[128,4,32]{0,2,1:T(8,128)}), f32[128,4,32]{0,2,1:T(8,128)S(1)}, u32[]{:S(2)}, u32[]{:S(2)}) async-start(f32[128,4,32]{0,2,1:T(8,128)} %bitcast), calls=%async_computation | async-start | bytes 131072 | tf_op jit(solution)/shard_map/all_to_all | solution.py:17
  12.3 28.8 %all-to-all-start.1 = ((bf16[32,128,128]{1,0,2:T(8,128)(2,1)}), bf16[32,128,128]{1,0,2:T(8,128)(2,1)S(1)}, u32[]{:S(2)}, u32[]{:S(2)}) async-start(bf16[32,128,128]{1,0,2:T(8,128)(2,1)} %copy.26), calls=%async_computation.1 | async-start | bytes 2097152 | tf_op jit(solution)/shard_map/all_to_all | solution.py:16
  47.5 3.7 %copy-start = (f32[8]{0:T(128)S(1)}, f32[8]{0:T(128)}, u32[]{:S(2)}) copy-start(f32[8]{0:T(128)} %param.9) | copy-start | bytes 100
where the time goes:
time: 172 us; the launch traced here: 171 us
  blocking collectives  61.8 us (36%)
  other arithmetic  61.1 us (36%)
  waiting for transfers between devices  23.1 us (13%)
  starting transfers between devices  8.92 us (5%)
  local copies, waits for them, and re-layouts  8.63 us (5%)
  matrix products  6.48 us (4%)
    psum x3, blocking collectives, shards(): slot_share = lax.psum(share_terms, 'draw') / total_draws  44.3 us
    all_to_all x1, waiting for transfers between devices, shards(): lax.all_to_all(features, 'mkt', split_axis=2, concat_axis=1, tiled=True)  22 us
    mul x3, other arithmetic, shards(): grouped * nest_ratio[:, :, None, :]  20.1 us
    psum x3, blocking collectives, shards(): totals = lax.psum(jnp.sum(inclusive_value, axis=1), 'nest')  17.4 us
    mul x2, other arithmetic, shards(): live_flag[None, :, None]  13.6 us
    reduce_sum x3, other arithmetic, shards(): jnp.sum(grouped * nest_ratio[:, :, None, :], axis=3)  13.4 us
    reduce_sum x3, other arithmetic, shards(): inner_sum = jnp.sum(grouped, axis=2)  11 us
    dot_general x1, matrix products, shards(): jnp.einsum('dve,dvb->deb', slot_features, taste_matrix, preferred_element...  6.48 us
  transfers between devices with their start and end apart: 2, of which 2 were waited for; matrix products, arithmetic and copies ran while one was open for 4% of the time, Pallas kernels for 0%

commit v1 on v0

--- a/solution.py
+++ b/solution.py
@@ -56,7 +56,7 @@
         share_terms = jnp.sum(grouped * nest_ratio[:, :, None, :], axis=3).reshape(
             market_list, columns
         )
-        slot_share = lax.psum(share_terms, "draw") / total_draws
+        slot_share = jnp.sum(lax.all_gather(share_terms, "draw"), axis=0) / total_draws
         value_slot = revise(value_slot, slot_share, slot_log, nest_rate, occupied)
     return (value_slot, slot_share)
 

time: 172 us -> 152 us (0.88)
  blocking collectives: 61.8 us -> 41.7 us
    psum x3 -> x0, blocking collectives: 44.3 us -> none  [shards(): slot_share = lax.psum(share_terms, 'draw') / total_draws]
    all_gather x0 -> x3, blocking collectives: none -> 24.3 us  [shards(): lax.all_gather(share_terms, 'draw')]
where the time goes in v1:
time: 152 us; the launch traced here: 151 us
  other arithmetic  61.2 us (40%)
  blocking collectives  41.7 us (27%)
  waiting for transfers between devices  23.1 us (15%)
  starting transfers between devices  8.92 us (6%)
  local copies, waits for them, and re-layouts  8.63 us (6%)
  matrix products  6.48 us (4%)
    all_gather x3, blocking collectives, shards(): lax.all_gather(share_terms, 'draw')  24.3 us
    all_to_all x1, waiting for transfers between devices, shards(): lax.all_to_all(features, 'mkt', split_axis=2, concat_axis=1, tiled=True)  22 us
    mul x3, other arithmetic, shards(): grouped * nest_ratio[:, :, None, :]  20.1 us
    psum x3, blocking collectives, shards(): totals = lax.psum(jnp.sum(inclusive_value, axis=1), 'nest')  17.4 us
    mul x2, other arithmetic, shards(): live_flag[None, :, None]  13.6 us
    reduce_sum x3, other arithmetic, shards(): jnp.sum(grouped * nest_ratio[:, :, None, :], axis=3)  13.4 us
    reduce_sum x3, other arithmetic, shards(): inner_sum = jnp.sum(grouped, axis=2)  11 us
    dot_general x1, matrix products, shards(): jnp.einsum('dve,dvb->deb', slot_features, taste_matrix, preferred_element...  6.48 us
  transfers between devices with their start and end apart: 2, of which 2 were waited for; matrix products, arithmetic and copies ran while one was open for 4% of the time, Pallas kernels for 0%

profile of v1, /device:TPU:1, one launch (start us, length us, event | category | flops | bytes accessed | tf_op | source)
XLA Modules:
  0.0 150.8 jit_solution(1232502129095779570)
XLA Ops:
  0.7 1.6 %copy.34 = f32[128,128]{0,1:T(8,128)} copy(f32[128,128]{1,0:T(8,128)} %param.11) | data formatting | bytes 131072 | tf_op args[5]
  2.2 5.4 %all-to-all-start = ((f32[128,4,32]{0,2,1:T(8,128)}), f32[128,4,32]{0,2,1:T(8,128)S(1)}, u32[]{:S(2)}, u32[]{:S(2)}) async-start(f32[128,4,32]{0,2,1:T(8,128)} %bitcast), calls=%async_computation | async-start | bytes 131072 | tf_op jit(solution)/shard_map/all_to_all | solution.py:17
  8.5 2.7 %copy.37 = bf16[32,128,128]{1,0,2:T(8,128)(2,1)} copy(bf16[32,128,128]{2,1,0:T(8,128)(2,1)} %param.6) | data formatting | bytes 2097152 | tf_op args[0]
  12.3 3.5 %all-to-all-start.1 = ((bf16[32,128,128]{1,0,2:T(8,128)(2,1)}), bf16[32,128,128]{1,0,2:T(8,128)(2,1)S(1)}, u32[]{:S(2)}, u32[]{:S(2)}) async-start(bf16[32,128,128]{1,0,2:T(8,128)(2,1)} %copy.37), calls=%async_computation.1 | async-start | bytes 2097152 | tf_op jit(solution)/shard_map/all_to_all | solution.py:16
  17.5 1.1 gather_fusion
  19.1 22.0 %all-to-all-done.1 = bf16[32,128,128]{1,0,2:T(8,128)(2,1)S(1)} async-done(((bf16[32,128,128]{1,0,2:T(8,128)(2,1)}), bf16[32,128,128]{1,0,2:T(8,128)(2,1)S(1)}, u32[]{:S(2)}, u32[]{:S(2)}) %all-to-all-start.1) | async-done | bytes 1048608 | tf_op jit(solution)/shard_map/all_to_all | solution.py:16
  41.0 6.5 %exponential_multiply_fusion.2 = (f32[32,384,128]{2,1,0:T(8,128)}, f32[32,384,128]{2,1,0:T(8,128)}) fusion(f32[384]{0:T(512)S(1)} %reshape.106, f32[32,384]{1,0:T(8,128)S(1)} %copy.36, f32[384]{0:T(512)S(1)} %convert_element_type.20, bf16[32,32,128]{2,1,0:T(8,128)(2,1)S(1)} %copy-done.1, f32[32]{0:T(128)S(1)} %copy-done.2, ...), kind=kOutput, calls=%fused_computation.6 | convolution fusion | flops 509214720 | bytes 13947904 | tf_op jit(solution)/shard_map/dve,dvb->deb/dot_general | solution.py:43
  47.5 3.7 %reduce_sum.118 = f32[32,8,128]{2,1,0:T(8,128)S(1)} reduce(f32[32,8,48,128]{3,2,1,0:T(8,128)} %bitcast.65, f32[]{:T(128)} %constant.28.clone.1), dimensions={2}, to_apply=%region_1.2 | reduce | flops 1540096 | bytes 6422532 | tf_op jit(solution)/shard_map/reduce_sum | solution.py:52
  51.3 6.1 %psum.21 = f32[32,128]{1,0:T(8,128)S(1)} all-reduce(f32[32,128]{1,0:T(8,128)S(1)} %fusion.27), channel_id=1, replica_groups=mesh['mkt'=4,'draw'=4,'nest'=2] {'nest'}, use_global_device_ids=true, to_apply=%region_3.4 | all-reduce | flops 4096 | bytes 32768 | tf_op jit(solution)/shard_map/psum | solution.py:54
  57.5 6.2 %bitcast_multiply_fusion.2 = f32[32,384,128]{2,1,0:T(8,128)} fusion(f32[32,384,128]{2,1,0:T(8,128)} %get-tuple-element.12, f32[32,8,128]{2,1,0:T(8,128)S(1)} %multiply_divide_fusion.2), kind=kLoop, calls=%fused_computation.3 | loop fusion | flops 1572864 | bytes 12713984 | tf_op jit(solution)/shard_map/mul | solution.py:56
  63.8 4.5 %reduce_sum.120 = f32[32,384]{1,0:T(8,128)S(1)} reduce(f32[32,384,128]{2,1,0:T(8,128)} %bitcast_multiply_fusion.2, f32[]{:T(128)} %constant.28.clone.1), dimensions={2}, to_apply=%region_4.5 | reduce | flops 1560576 | bytes 6340612 | tf_op jit(solution)/shard_map/reduce_sum | solution.py:56
  68.2 8.9 %all-gather = f32[128,384]{1,0:T(8,128)S(1)} all-gather(f32[32,384]{1,0:T(8,128)S(1)} %reduce_sum.120), channel_id=2, replica_groups=mesh['mkt'=4,'draw'=4,'nest'=2] {'draw'}, dimensions={0}, use_global_device_ids=true | all-gather | bytes 245760 | tf_op jit(solution)/shard_map/all_gather | solution.py:59
  77.6 6.8 %exponential_multiply_fusion.1 = f32[32,384,128]{2,1,0:T(8,128)} fusion(f32[32,384,128]{2,1,0:T(8,128)} %get-tuple-element.13, f32[32,384]{1,0:T(8,128)S(1)} %copy.42, f32[384]{0:T(512)S(1)} %reshape.106, f32[384]{0:T(512)S(1)} %convert_element_type.20), kind=kLoop, calls=%fused_computation.5 | loop fusion | flops 4718592 | bytes 12635136 | tf_op jit(solution)/shard_map/mul | solution.py:48
  84.4 3.7 %reduce_sum.122 = f32[32,8,128]{2,1,0:T(8,128)S(1)} reduce(f32[32,8,48,128]{3,2,1,0:T(8,128)} %bitcast.66, f32[]{:T(128)} %constant.28.clone.1), dimensions={2}, to_apply=%region_6.7 | reduce | flops 1540096 | bytes 6422532 | tf_op jit(solution)/shard_map/reduce_sum | solution.py:52
  88.2 5.2 %psum.22 = f32[32,128]{1,0:T(8,128)S(1)} all-reduce(f32[32,128]{1,0:T(8,128)S(1)} %fusion.26), channel_id=1, replica_groups=mesh['mkt'=4,'draw'=4,'nest'=2] {'nest'}, use_global_device_ids=true, to_apply=%region_8.9 | all-reduce | flops 4096 | bytes 32768 | tf_op jit(solution)/shard_map/psum | solution.py:54
  93.4 6.9 %bitcast_multiply_fusion.1 = f32[32,384,128]{2,1,0:T(8,128)} fusion(f32[32,8,128]{2,1,0:T(8,128)S(1)} %multiply_divide_fusion.1, f32[384]{0:T(512)S(1)} %reshape.106, f32[32,384,128]{2,1,0:T(8,128)} %get-tuple-element.13, f32[32,384]{1,0:T(8,128)S(1)} %copy.42, f32[384]{0:T(512)S(1)} %convert_element_type.20), kind=kLoop, calls=%fused_computation.2 | loop fusion | flops 6291456 | bytes 12766208 | tf_op jit(solution)/shard_map/mul | solution.py:56
  100.4 4.5 %reduce_sum.124 = f32[32,384]{1,0:T(8,128)S(1)} reduce(f32[32,384,128]{2,1,0:T(8,128)} %bitcast_multiply_fusion.1, f32[]{:T(128)} %constant.28.clone.1), dimensions={2}, to_apply=%region_9.10 | reduce | flops 1560576 | bytes 6340612 | tf_op jit(solution)/shard_map/reduce_sum | solution.py:56
  104.8 7.8 %all-gather.1 = f32[128,384]{1,0:T(8,128)S(1)} all-gather(f32[32,384]{1,0:T(8,128)S(1)} %reduce_sum.124), channel_id=3, replica_groups=mesh['mkt'=4,'draw'=4,'nest'=2] {'draw'}, dimensions={0}, use_global_device_ids=true | all-gather | bytes 245760 | tf_op jit(solution)/shard_map/all_gather | solution.py:59
  113.1 6.8 %exponential_multiply_fusion = f32[32,384,128]{2,1,0:T(8,128)} fusion(f32[32,384,128]{2,1,0:T(8,128)} %get-tuple-element.13, f32[32,384]{1,0:T(8,128)S(1)} %copy.44, f32[384]{0:T(512)S(1)} %reshape.106, f32[384]{0:T(512)S(1)} %convert_element_type.20), kind=kLoop, calls=%fused_computation.4 | loop fusion | flops 4718592 | bytes 12635136 | tf_op jit(solution)/shard_map/mul | solution.py:48
  119.9 3.7 %reduce_sum.126 = f32[32,8,128]{2,1,0:T(8,128)S(1)} reduce(f32[32,8,48,128]{3,2,1,0:T(8,128)} %bitcast.67, f32[]{:T(128)} %constant.28.clone.1), dimensions={2}, to_apply=%region_11.12 | reduce | flops 1540096 | bytes 6422532 | tf_op jit(solution)/shard_map/reduce_sum | solution.py:52
  123.7 6.1 %psum.23 = f32[32,128]{1,0:T(8,128)S(1)} all-reduce(f32[32,128]{1,0:T(8,128)S(1)} %fusion.25), channel_id=1, replica_groups=mesh['mkt'=4,'draw'=4,'nest'=2] {'nest'}, use_global_device_ids=true, to_apply=%region_13.14 | all-reduce | flops 4096 | bytes 32768 | tf_op jit(solution)/shard_map/psum | solution.py:54
  129.9 6.9 %bitcast_multiply_fusion = f32[32,384,128]{2,1,0:T(8,128)} fusion(f32[32,8,128]{2,1,0:T(8,128)S(1)} %multiply_divide_fusion, f32[384]{0:T(512)S(1)} %reshape.106, f32[32,384,128]{2,1,0:T(8,128)} %get-tuple-element.13, f32[32,384]{1,0:T(8,128)S(1)} %copy.44, f32[384]{0:T(512)S(1)} %convert_element_type.20), kind=kLoop, calls=%fused_computation.1 | loop fusion | flops 6291456 | bytes 12766208 | tf_op jit(solution)/shard_map/mul | solution.py:56
  136.9 4.5 %reduce_sum.128 = f32[32,384]{1,0:T(8,128)S(1)} reduce(f32[32,384,128]{2,1,0:T(8,128)} %bitcast_multiply_fusion, f32[]{:T(128)} %constant.28.clone.1), dimensions={2}, to_apply=%region_14.15 | reduce | flops 1560576 | bytes 6340612 | tf_op jit(solution)/shard_map/reduce_sum | solution.py:56
  141.4 7.6 %all-gather.2 = f32[128,384]{1,0:T(8,128)S(1)} all-gather(f32[32,384]{1,0:T(8,128)S(1)} %reduce_sum.128), channel_id=4, replica_groups=mesh['mkt'=4,'draw'=4,'nest'=2] {'draw'}, dimensions={0}, use_global_device_ids=true | all-gather | bytes 245760 | tf_op jit(solution)/shard_map/all_gather | solution.py:59
  (44 shorter events, 7.4 us)
Async XLA Ops:
  0.6 40.4 %copy-start.1 = (bf16[32,32,128]{2,1,0:T(8,128)(2,1)S(1)}, bf16[32,32,128]{2,1,0:T(8,128)(2,1)}, u32[]{:S(2)}) copy-start(bf16[32,32,128]{2,1,0:T(8,128)(2,1)} %param.7) | copy-start | bytes 786436
  0.6 40.4 %copy-start.2 = (f32[32]{0:T(128)S(1)}, f32[32]{0:T(128)}, u32[]{:S(2)}) copy-start(f32[32]{0:T(128)} %param.8) | copy-start | bytes 388
  2.2 10.0 %all-to-all-start = ((f32[128,4,32]{0,2,1:T(8,128)}), f32[128,4,32]{0,2,1:T(8,128)S(1)}, u32[]{:S(2)}, u32[]{:S(2)}) async-start(f32[128,4,32]{0,2,1:T(8,128)} %bitcast), calls=%async_computation | async-start | bytes 131072 | tf_op jit(solution)/shard_map/all_to_all | solution.py:17
  12.3 28.8 %all-to-all-start.1 = ((bf16[32,128,128]{1,0,2:T(8,128)(2,1)}), bf16[32,128,128]{1,0,2:T(8,128)(2,1)S(1)}, u32[]{:S(2)}, u32[]{:S(2)}) async-start(bf16[32,128,128]{1,0,2:T(8,128)(2,1)} %copy.37), calls=%async_computation.1 | async-start | bytes 2097152 | tf_op jit(solution)/shard_map/all_to_all | solution.py:16
  47.5 3.7 %copy-start = (f32[8]{0:T(128)S(1)}, f32[8]{0:T(128)}, u32[]{:S(2)}) copy-start(f32[8]{0:T(128)} %param.9) | copy-start | bytes 100
